TPU v7x, 32 devices: a whole 2x2x4 slice. The times are simulated.
32 devices in a mesh: cells: 16 (over z, x, core), ens: 2 (over y).
Axes of the slice: x: 2, y: 2, z: 4, core: 2. Of those that a mesh axis runs over, the one named last changes fastest.
Arguments:
- later_adjoint: float32 [4, 4, 32, 8, 128], P('ens', None, 'cells'), may hold values from -6 to 6
- coupling: bfloat16 [4, 6, 4, 4, 32, 8, 128], P('ens', None, None, None, 'cells'), may hold values from -0.59765625 to 0.59765625
- diag_inverse: bfloat16 [4, 4, 4, 32, 8, 128], P('ens', None, None, 'cells'), may hold values from -0.7 to 1.6, as said below
- sensitivity: bfloat16 [4, 4, 32, 8, 128, 128], P('ens', None, 'cells'), may hold values from -0.0625 to 0.0625
- well_cells: int32 [256], replicated, may hold values from 0 to 32767
- well_misfit: float32 [4, 4, 256], P('ens'), may hold values from -6 to 6
- block_map: int32 [32, 8, 128], P('cells'), may hold values from 0 to 63, as said below
Outputs:
- adjoint: float32 [4, 4, 32, 8, 128], P('ens', None, 'cells')
- gradient: float32 [64, 128], P('cells')
Inputs may be any that keep to these rules, and one draw needn't show every extreme that they name: `block_map`: of the cells of each slab of 2 planes along the first dimension (x from i * 2 to i * 2 + 1), exactly 128 map to blocks whose number divided by 4 (rounded down) equals any given j. `diag_inverse`: each block is the inverse of a diagonal block; its diagonal entries lie in 0.4 to 1.6. `well_cells`: wells may share a cell.
All inputs are finite; a program needn't handle non-finite values.
Results may differ from a plain program's by a relative error of at most 0.0003.
Values sent between devices are 32-bit elements; how exact they have to be, the bound alone decides.
A program may use at most 64 MiB of HBM per device.

v0:
```python
import functools

import jax
import jax.numpy as jnp
from jax import lax
from jax.experimental import pallas as pl
from jax.experimental.pallas import tpu as pltpu
from jax.sharding import PartitionSpec as P

ITERS = 4
MESH = pl.DeviceIdType.MESH
F32 = jnp.float32
BF16 = jnp.bfloat16


def for_each(count, step):
    if count <= 64:
        for i in range(count):
            step(i)
    else:
        def body(i, carry):
            step(i)
            return carry

        lax.fori_loop(0, count, body, 0)


def split(value):
    high = value.astype(BF16).astype(F32)
    return high, value - high


def kernel(
    ranks, groups, blocks,
    later_hbm, coup_hbm, diag_hbm, sens_hbm, wells_hbm, misfit_hbm, map_hbm,
    adj, got_out,
    later, coup, diag, sens, wells, misfit, bmap, source,
    up_send, down_send, below, above, mask, lhs, part, got,
    load_sem, sens_sem, up_ssem, up_rsem, down_ssem, down_rsem, part_ssem, part_rsem, here_sem,
):
    members, unknowns, planes, columns, layers = later.shape
    rows = planes * columns
    count = rows * layers
    devices = ranks * groups
    blk_dev = blocks // ranks
    me_c = lax.axis_index("cells")
    me_e = lax.axis_index("ens")
    me = me_c * groups + me_e

    def other(step):
        at = me + step + 1
        at = jnp.where(at >= devices, at - devices, at)
        return at // groups, at % groups

    barrier = pltpu.get_barrier_semaphore()

    bits = devices.bit_length() - 1

    def partner(bit):
        size = 1 << bit
        at = me + size - 2 * size * ((me // size) % 2)
        return at // groups, at % groups

    beside = me_c + 2 * (me_c % 2) - 1
    has_beside = (beside >= 0) & (beside < ranks)

    def greet_all():
        @pl.when(has_beside)
        def _():
            pl.semaphore_signal(barrier, inc=1, device_id=(beside, me_e), device_id_type=MESH)

        for bit in range(bits):
            pl.semaphore_signal(barrier, inc=1, device_id=partner(bit), device_id_type=MESH)

    def greeted():
        pl.semaphore_wait(barrier, jnp.where(has_beside, bits + 1, bits))

    def tell(bit):
        if bit < bits:
            pl.semaphore_signal(here_sem.at[bit], inc=1, device_id=partner(bit), device_id_type=MESH)

    def hear(bit):
        if bit < bits:
            pl.semaphore_wait(here_sem.at[bit], 1)

    greet_all()
    loads = [
        pltpu.make_async_copy(src, dst, load_sem.at[i])
        for i, (src, dst) in enumerate(
            [
                (wells_hbm, wells), (misfit_hbm, misfit), (later_hbm, later), (diag_hbm, diag),
                (coup_hbm, coup), (map_hbm, bmap),
            ]
        )
    ]
    for load in loads:
        load.start()
    fields = members * unknowns
    sens_loads = [
        pltpu.make_async_copy(sens_hbm.at[i], sens.at[i], sens_sem.at[i]) for i in range(fields)
    ]

    loads[0].wait()
    loads[1].wait()
    total_wells = wells.shape[1]
    rel = wells[...] - me_c * count
    row_lo = lax.broadcasted_iota(jnp.int32, (rows, total_wells), 0) * layers
    in_row = (rel >= row_lo) & (rel < row_lo + layers)
    lane = wells[...] & (layers - 1)
    at_lane = lax.broadcasted_iota(jnp.int32, (layers, total_wells), 0) == lane
    at_lane = jnp.where(at_lane, 1.0, 0.0).astype(BF16)
    parts = [[], [], []]
    for m in range(members):
        for u in range(unknowns):
            rest = jnp.broadcast_to(misfit[m, u : u + 1, :], (rows, total_wells))
            rest = jnp.where(in_row, rest, 0.0)
            for i in range(3):
                high, rest = split(rest)
                parts[i].append(high.astype(BF16))
    injected = jnp.zeros((fields * rows, layers), F32)
    for piece in parts:
        injected = injected + lax.dot_general(
            jnp.concatenate(piece, axis=0), at_lane, (((1,), (1,)), ((), ())),
            preferred_element_type=F32,
        )
    loads[2].wait()
    source[...] = later[...] + injected.reshape(later.shape)

    def inverse(m, rhs):
        out = None
        for w in range(unknowns):
            term = diag[m, w].astype(F32) * rhs[w][None]
            out = term if out is None else out + term
        return out

    loads[3].wait()
    now = [inverse(m, source[m]) for m in range(members)]
    loads[4].wait()
    for load in sens_loads:
        load.start()

    first = me_c == 0
    last = me_c == ranks - 1
    next_id = (jnp.minimum(me_c + 1, ranks - 1), me_e)
    prev_id = (jnp.maximum(me_c - 1, 0), me_e)

    def up_copy(k, m):
        return pltpu.make_async_remote_copy(
            src_ref=up_send.at[k, m], dst_ref=below.at[k, m], send_sem=up_ssem.at[k, m],
            recv_sem=up_rsem.at[k, m], device_id=next_id, device_id_type=MESH,
        )

    def down_copy(k, m):
        return pltpu.make_async_remote_copy(
            src_ref=down_send.at[k, m], dst_ref=above.at[k, m], send_sem=down_ssem.at[k, m],
            recv_sem=down_rsem.at[k, m], device_id=prev_id, device_id_type=MESH,
        )

    @pl.when(first)
    def _():
        below[...] = jnp.zeros_like(below)

    @pl.when(last)
    def _():
        above[...] = jnp.zeros_like(above)

    lane_at = lax.broadcasted_iota(jnp.int32, (unknowns, planes, columns, layers), 3)
    col_at = lax.broadcasted_iota(jnp.int32, (unknowns, planes, columns, layers), 2)

    def product(m, k, value, lo, hi):
        out = None
        for u in range(unknowns):
            term = coup[m, k, u, :, lo:hi].astype(F32) * value[u, lo:hi][None]
            out = term if out is None else out + term
        return out

    def edges(k, m, value):
        up_send[k, m] = product(m, 0, value, planes - 1, planes)[:, 0]
        down_send[k, m] = product(m, 1, value, 0, 1)[:, 0]

    def send(k, m):
        @pl.when(jnp.logical_not(last))
        def _():
            up_copy(k, m).start()

        @pl.when(jnp.logical_not(first))
        def _():
            down_copy(k, m).start()

    def inside(m, value):
        up = product(m, 0, value, 0, planes - 1)
        down = product(m, 1, value, 1, planes)
        moved = pltpu.roll(product(m, 2, value, 0, planes), 1, 2)
        total = jnp.where(col_at == 0, 0.0, moved)
        moved = pltpu.roll(product(m, 3, value, 0, planes), columns - 1, 2)
        total = total + jnp.where(col_at == columns - 1, 0.0, moved)
        moved = pltpu.roll(product(m, 4, value, 0, planes), 1, 3)
        total = total + jnp.where(lane_at == 0, 0.0, moved)
        moved = pltpu.roll(product(m, 5, value, 0, planes), layers - 1, 3)
        total = total + jnp.where(lane_at == layers - 1, 0.0, moved)
        return source[m] - total, up, down

    for m in range(members):
        edges(0, m, now[m])
    greeted()
    for m in range(members):
        send(0, m)
    tell(0)
    for k in range(ITERS):
        inner = [inside(m, now[m]) for m in range(members)]
        if k == 0:
            loads[5].wait()
            ids = lax.broadcasted_iota(jnp.int32, (blocks, layers), 0)
            for x in range(planes):
                for y in range(columns):
                    row = x * columns + y
                    hit = jnp.where(bmap[x, y : y + 1, :] == ids, 1.0, 0.0)
                    mask[:, row * layers : (row + 1) * layers] = hit.astype(BF16)
        after = []
        for m in range(members):
            rest, up, down = inner[m]

            @pl.when(jnp.logical_not(first))
            def _(m=m):
                up_copy(k, m).wait_recv()

            @pl.when(jnp.logical_not(last))
            def _(m=m):
                down_copy(k, m).wait_recv()

            rest = rest - jnp.concatenate([below[k, m][:, None], up], axis=1)
            rest = rest - jnp.concatenate([down, above[k, m][:, None]], axis=1)
            value = inverse(m, rest)
            if k < ITERS - 1:
                edges(k + 1, m, value)
                send(k + 1, m)
            else:
                adj[m] = value
            after.append(value)
        now = after
        hear(k)
        tell(k + 1)

    def gather(i, total):
        pltpu.make_async_copy(sens_hbm.at[i], sens.at[i], sens_sem.at[i]).wait()
        high, low = split(adj[i // unknowns, i % unknowns])
        slot = i % 2
        for x in range(planes):
            for y in range(columns):
                row = x * columns + y
                cols = slice(row * layers, (row + 1) * layers)
                hot = mask[:, cols]
                for j, value in enumerate((high, low)):
                    wide = jnp.broadcast_to(value[x, y : y + 1], (16, layers)).astype(BF16)
                    wide = jnp.concatenate([wide] * (blocks // 16), axis=0)
                    lhs[slot, j * blocks : (j + 1) * blocks, cols] = hot * wide
        return total + jnp.dot(
            lhs[slot], sens[i].reshape(count, sens.shape[-1]), preferred_element_type=F32
        )

    total = jnp.zeros((2 * blocks, sens.shape[-1]), F32)
    total = lax.fori_loop(0, fields, gather, total, unroll=blocks <= 64)
    total = total[:blocks] + total[blocks:]
    for c in range(ranks):
        part[c] = total[c * blk_dev : (c + 1) * blk_dev]

    def part_copy(step):
        c, e = other(step)
        return pltpu.make_async_remote_copy(
            src_ref=part.at[c], dst_ref=got.at[step], send_sem=part_ssem, recv_sem=part_rsem,
            device_id=(c, e), device_id_type=MESH,
        )

    hear(ITERS)
    for bit in range(ITERS + 1, bits):
        tell(bit)
        hear(bit)
    for_each(devices - 1, lambda step: part_copy(step).start())
    everything = pltpu.make_async_remote_copy(
        src_ref=got, dst_ref=got, send_sem=part_ssem, recv_sem=part_rsem,
        device_id=next_id, device_id_type=MESH,
    )
    everything.wait_recv()
    got_out[...] = part[me_c] + jnp.sum(got[...], axis=0)

    everything.wait_send()
    for k in range(ITERS):
        for m in range(members):
            @pl.when(jnp.logical_not(last))
            def _(k=k, m=m):
                up_copy(k, m).wait_send()

            @pl.when(jnp.logical_not(first))
            def _(k=k, m=m):
                down_copy(k, m).wait_send()


def write_out(adjoint, gradient, adjoint_hbm, gradient_hbm, sem):
    copies = [
        pltpu.make_async_copy(adjoint, adjoint_hbm, sem.at[0]),
        pltpu.make_async_copy(gradient, gradient_hbm, sem.at[1]),
    ]
    for copy in copies:
        copy.start()
    for copy in copies:
        copy.wait()


def solution(mesh):
    ranks, groups = mesh.shape["cells"], mesh.shape["ens"]
    assert (ranks * groups) & (ranks * groups - 1) == 0

    def body(later_adjoint, coupling, diag_inverse, sensitivity, well_cells, well_misfit, block_map):
        members, unknowns, planes, columns, layers = later_adjoint.shape
        params = sensitivity.shape[-1]
        rows = planes * columns
        blk_dev = 4
        blocks = ranks * blk_dev
        fields = members * unknowns
        sens = sensitivity.reshape(fields, rows, layers, params)
        wells = well_cells.reshape(1, -1)
        halo = (ITERS, members, unknowns, columns, layers)
        any_spec = pl.BlockSpec(memory_space=pl.ANY)
        vmem_spec = pl.BlockSpec(memory_space=pltpu.VMEM)
        dma = pltpu.SemaphoreType.DMA
        adjoint, gradient = pl.pallas_call(
            functools.partial(kernel, ranks, groups, blocks),
            out_shape=(
                pltpu.VMEM(later_adjoint.shape, F32),
                pltpu.VMEM((blk_dev, params), F32),
            ),
            in_specs=[any_spec] * 7,
            out_specs=(vmem_spec, vmem_spec),
            scratch_shapes=[
                pltpu.VMEM(later_adjoint.shape, F32),
                pltpu.VMEM(coupling.shape, BF16),
                pltpu.VMEM(diag_inverse.shape, BF16),
                pltpu.VMEM(sens.shape, BF16),
                pltpu.VMEM(wells.shape, jnp.int32),
                pltpu.VMEM(well_misfit.shape, F32),
                pltpu.VMEM(block_map.shape, jnp.int32),
                pltpu.VMEM(later_adjoint.shape, F32),
                pltpu.VMEM(halo, F32),
                pltpu.VMEM(halo, F32),
                pltpu.VMEM(halo, F32),
                pltpu.VMEM(halo, F32),
                pltpu.VMEM((blocks, rows * layers), BF16),
                pltpu.VMEM((2, 2 * blocks, rows * layers), BF16),
                pltpu.VMEM((ranks, blk_dev, params), F32),
                pltpu.VMEM((ranks * groups - 1, blk_dev, params), F32),
                dma((6,)),
                dma((fields,)),
                dma((ITERS, members)),
                dma((ITERS, members)),
                dma((ITERS, members)),
                dma((ITERS, members)),
                dma,
                dma,
                pltpu.SemaphoreType.REGULAR(((ranks * groups).bit_length() - 1,)),
            ],
            compiler_params=pltpu.CompilerParams(collective_id=0, has_side_effects=True),
        )(later_adjoint, coupling, diag_inverse, sens, wells, well_misfit, block_map)
        return pl.pallas_call(
            write_out,
            out_shape=(
                jax.ShapeDtypeStruct(adjoint.shape, F32),
                jax.ShapeDtypeStruct(gradient.shape, F32),
            ),
            in_specs=[vmem_spec] * 2,
            out_specs=(any_spec, any_spec),
            scratch_shapes=[dma((2,))],
        )(*[pltpu.with_memory_space_constraint(a, pltpu.VMEM) for a in (adjoint, gradient)])

    placed = (
        P("ens", None, "cells", None, None),
        P("ens", None, None, None, "cells", None, None),
        P("ens", None, None, "cells", None, None),
        P("ens", None, "cells", None, None, None),
        P(),
        P("ens", None, None),
        P("cells", None, None),
    )
    return jax.shard_map(
        body,
        mesh=mesh,
        in_specs=placed,
        out_specs=(P("ens", None, "cells", None, None), P("cells", None)),
        check_vma=False,
    )
```

profile of v0, /device:TPU:0, one launch (start us, length us, event | category | flops | bytes accessed | tf_op | source)
XLA Modules:
  0.0 24.9 jit_solution(8079713817004415141)
XLA Ops:
  0.6 23.6 %shard_map.86 = (f32[2,4,2,8,128]{4,3,2,1,0:T(8,128)S(1)}, f32[4,128]{1,0:T(4,128)S(1)}) custom-call(f32[2,4,2,8,128]{4,3,2,1,0:T(8,128)} %later_hbm.1, bf16[2,6,4,4,2,8,128]{6,5,4,3,2,1,0:T(8,128)(2,1)} %coup_hbm.1, bf16[2,4,4,2,8,128]{5,4,3,2,1,0:T(8,128)(2,1)} %diag_hbm.1, bf16[8,16,128,128]{3,2,1,0:T(8,128)(2,1)} %bitcast.2, s32[1,256]{1,0:T(1,128)} %bitcast.3, ...), custom_call_target="tpu_custom_call" | custom-call | tf_op jit(solution)/shard_map/pallas_call | solution.py:326
  24.2 0.7 %shard_map.87 = (f32[2,4,2,8,128]{4,3,2,1,0:T(8,128)}, f32[4,128]{1,0:T(4,128)}) custom-call(f32[2,4,2,8,128]{4,3,2,1,0:T(8,128)S(1)} %get-tuple-element.4.adjoint, f32[4,128]{1,0:T(4,128)S(1)} %get-tuple-element.5.gradient), custom_call_target="tpu_custom_call" | custom-call | tf_op jit(solution)/shard_map/pallas_call | solution.py:363
where the time goes:
time: 25 us; the launch traced here: 24.9 us
  Pallas kernels  24.2 us (97%)
  between operations  0.64 us (3%)
    pallas_call x1, Pallas kernels, body(): pl.pallas_call(functools.partial(kernel, ranks, groups, blocks), out_shap...  23.6 us
    pallas_call x1, Pallas kernels, body(): pl.pallas_call(write_out, out_shape=(jax.ShapeDtypeStruct(adjoint.shape,...  0.65 us

commit v1 on v0

v1 whole, which is shorter than its diff:
```python
import functools

import jax
import jax.numpy as jnp
from jax import lax
from jax.experimental import pallas as pl
from jax.experimental.pallas import tpu as pltpu
from jax.sharding import PartitionSpec as P

ITERS = 4
MESH = pl.DeviceIdType.MESH
F32 = jnp.float32
BF16 = jnp.bfloat16


def for_each(count, step):
    if count <= 64:
        for i in range(count):
            step(i)
    else:
        def body(i, carry):
            step(i)
            return carry

        lax.fori_loop(0, count, body, 0)


def split(value):
    high = value.astype(BF16).astype(F32)
    return high, value - high


def kernel(
    ranks, groups, blocks,
    later_hbm, coup_hbm, diag_hbm, sens_hbm, wells_hbm, misfit_hbm, map_hbm,
    adj, got_out,
    later, coup, diag, sens, wells, misfit, bmap, source,
    out_buf, in_buf, mid_edge, last_edge, left, mask, part, got,
    load_sem, recv_sem, send_sem, part_ssem, part_rsem, here_sem,
):
    members, unknowns, planes, columns, layers = later.shape
    rows = planes * columns
    count = rows * layers
    devices = ranks * groups
    blk_dev = blocks // ranks
    fields = members * unknowns
    me_c = lax.axis_index("cells")
    me_e = lax.axis_index("ens")
    me = me_c * groups + me_e
    assert planes >= 2

    loads = [
        pltpu.make_async_copy(src, dst, load_sem.at[i])
        for i, (src, dst) in enumerate(
            [
                (wells_hbm, wells), (misfit_hbm, misfit), (later_hbm, later), (diag_hbm, diag),
                (coup_hbm.at[:, 0:2], coup.at[:, 0:2]), (coup_hbm.at[:, 2:6], coup.at[:, 2:6]),
                (map_hbm, bmap), (sens_hbm, sens),
            ]
        )
    ]
    for load in loads[:7]:
        load.start()

    barrier = pltpu.get_barrier_semaphore()
    block_c = 1
    while (block_c * groups) ** 2 < devices:
        block_c *= 2
    columns_c = ranks // block_c

    def wrap(at, size):
        return jnp.where(at >= size, at - size, at)

    pos_c = lax.rem(me_c, block_c)
    base_c = me_c - pos_c
    near = [
        (base_c + wrap(pos_c + dc, block_c), wrap(me_e + de, groups))
        for dc in range(block_c) for de in range(groups) if dc or de
    ]
    far = [(wrap(me_c + block_c * s, ranks), me_e) for s in range(1, columns_c)]
    cross_up = (pos_c == block_c - 1) & (me_c < ranks - 1)
    cross_down = (pos_c == 0) & (me_c > 0)
    next_id = (jnp.minimum(me_c + 1, ranks - 1), me_e)
    prev_id = (jnp.maximum(me_c - 1, 0), me_e)

    def greet(who):
        pl.semaphore_signal(barrier, inc=1, device_id=who, device_id_type=MESH)

    for who in near + far:
        greet(who)

    @pl.when(cross_up)
    def _():
        greet(next_id)

    @pl.when(cross_down)
    def _():
        greet(prev_id)

    def greeted():
        extra = jnp.where(cross_up, 1, 0) + jnp.where(cross_down, 1, 0)
        pl.semaphore_wait(barrier, len(near) + len(far) + extra)

    has = (me_c > 0, me_c < ranks - 1)
    target = (prev_id, next_id)
    edge_at = (0, planes - 1)
    turn = lax.rem(me_c, 4)
    patient = (turn == 2, turn == 1)
    GAIN = 4

    def remote(d, src, dst, sem):
        return pltpu.make_async_remote_copy(
            src_ref=src, dst_ref=dst, send_sem=send_sem.at[d], recv_sem=sem,
            device_id=target[d], device_id_type=MESH,
        )

    def value_copy(d, slot, m):
        return remote(d, out_buf.at[d, slot, m], in_buf.at[1 - d, slot, m], recv_sem.at[1 - d, slot, m])

    def gain_copy(d, m):
        both = pl.ds(GAIN, unknowns)
        return remote(d, out_buf.at[d, both, m], in_buf.at[1 - d, both, m], recv_sem.at[1 - d, GAIN, m])

    def value_wait(d, slot, m):
        pltpu.make_async_remote_copy(
            src_ref=out_buf.at[d, slot, m], dst_ref=in_buf.at[d, slot, m], send_sem=send_sem.at[d],
            recv_sem=recv_sem.at[d, slot, m], device_id=next_id, device_id_type=MESH,
        ).wait_recv()

    def gain_wait(d, m):
        both = pl.ds(GAIN, unknowns)
        pltpu.make_async_remote_copy(
            src_ref=out_buf.at[d, both, m], dst_ref=in_buf.at[d, both, m], send_sem=send_sem.at[d],
            recv_sem=recv_sem.at[d, GAIN, m], device_id=next_id, device_id_type=MESH,
        ).wait_recv()

    for d in range(2):
        @pl.when(jnp.logical_not(has[d]))
        def _(d=d):
            in_buf[d] = jnp.zeros(in_buf.shape[1:], F32)

    loads[0].wait()
    loads[1].wait()
    total_wells = wells.shape[1]
    rel = wells[...] - me_c * count
    row_lo = lax.broadcasted_iota(jnp.int32, (rows, total_wells), 0) * layers
    in_row = (rel >= row_lo) & (rel < row_lo + layers)
    lane = wells[...] & (layers - 1)
    at_lane = lax.broadcasted_iota(jnp.int32, (layers, total_wells), 0) == lane
    at_lane = jnp.where(at_lane, 1.0, 0.0).astype(BF16)
    parts = [[], [], []]
    for m in range(members):
        for u in range(unknowns):
            rest = jnp.broadcast_to(misfit[m, u : u + 1, :], (rows, total_wells))
            rest = jnp.where(in_row, rest, 0.0)
            for i in range(3):
                high, rest = split(rest)
                parts[i].append(high.astype(BF16))
    injected = jnp.zeros((fields * rows, layers), F32)
    for piece in parts:
        injected = injected + lax.dot_general(
            jnp.concatenate(piece, axis=0), at_lane, (((1,), (1,)), ((), ())),
            preferred_element_type=F32,
        )
    loads[2].wait()
    source[...] = later[...] + injected.reshape(later.shape)

    def weighed(weights, values):
        out = None
        for w in range(unknowns):
            term = weights(w) * values[w][None]
            out = term if out is None else out + term
        return out

    def inverse(m, rhs):
        return weighed(lambda w: diag[m, w].astype(F32), rhs)

    loads[3].wait()
    loads[4].wait()

    def own_gain(d, m, values):
        return weighed(lambda w: out_buf[d, GAIN + w, m], values)

    def far_gain(d, m, values):
        return weighed(lambda w: in_buf[d, GAIN + w, m], values)

    for m in range(members):
        for d in range(2):
            at = edge_at[d]
            for w in range(unknowns):
                out_buf[d, GAIN + w, m] = weighed(
                    lambda u: coup[m, 1 - d, u, :, at].astype(F32), diag[m, w, :, at].astype(F32)
                )
    edge = [[None, None] for _ in range(members)]
    for m in range(members):
        for d in range(2):
            edge[m][d] = own_gain(d, m, source[m, :, edge_at[d]])
            out_buf[d, 0, m] = edge[m][d]
    greeted()

    def send(d, copy, when):
        @pl.when(has[d] & when if when is not None else has[d])
        def _():
            copy.start()

    hasty = tuple(jnp.logical_not(p) for p in patient)
    for m in range(members):
        for d in range(2):
            send(d, value_copy(d, 0, m), None)
    for m in range(members):
        for d in range(2):
            send(d, gain_copy(d, m), hasty[d])
    for who in far:
        pl.semaphore_signal(here_sem, inc=1, device_id=who, device_id_type=MESH)

    now = [inverse(m, source[m]) for m in range(members)]

    lane_at = lax.broadcasted_iota(jnp.int32, (unknowns, planes, columns, layers), 3)
    col_at = lax.broadcasted_iota(jnp.int32, (unknowns, planes, columns, layers), 2)

    def product(m, k, value, lo, hi):
        return weighed(lambda u: coup[m, k, u, :, lo:hi].astype(F32), value[:, lo:hi])

    def inside(m, value):
        moved = pltpu.roll(product(m, 2, value, 0, planes), 1, 2)
        total = jnp.where(col_at == 0, 0.0, moved)
        moved = pltpu.roll(product(m, 3, value, 0, planes), columns - 1, 2)
        total = total + jnp.where(col_at == columns - 1, 0.0, moved)
        moved = pltpu.roll(product(m, 4, value, 0, planes), 1, 3)
        total = total + jnp.where(lane_at == 0, 0.0, moved)
        moved = pltpu.roll(product(m, 5, value, 0, planes), layers - 1, 3)
        total = total + jnp.where(lane_at == layers - 1, 0.0, moved)
        up = product(m, 0, value, 0, planes - 1)
        down = product(m, 1, value, 1, planes)
        nothing = jnp.zeros((unknowns, 1, columns, layers), F32)
        total = total + jnp.concatenate([nothing, up], axis=1)
        total = total + jnp.concatenate([down, nothing], axis=1)
        return source[m] - total

    def ahead(d, slot, m, rest):
        out_buf[d, slot, m] = own_gain(d, m, rest[:, edge_at[d]])

    def subtract(rest, below, above):
        first_plane = rest[:, 0] - below
        last_plane = rest[:, planes - 1] - above
        return jnp.concatenate(
            [first_plane[:, None], rest[:, 1 : planes - 1], last_plane[:, None]], axis=1
        ) if planes > 2 else jnp.stack([first_plane, last_plane], axis=1)

    loads[5].wait()
    loads[7].start()
    rest = [inside(m, now[m]) for m in range(members)]
    for m in range(members):
        for d in range(2):
            @pl.when(hasty[d])
            def _(d=d, m=m):
                ahead(d, 1, m, rest[m])

            send(d, value_copy(d, 1, m), hasty[d])

    loads[6].wait()
    ids = lax.broadcasted_iota(jnp.int32, (blocks, layers), 0)
    for x in range(planes):
        for y in range(columns):
            hit = jnp.where(bmap[x, y : y + 1, :] == ids, 1.0, 0.0)
            mask[x, y] = hit.astype(BF16)

    first_edge = edge
    second_edge = [[None, None] for _ in range(members)]
    for m in range(members):
        for d in range(2):
            @pl.when(has[d])
            def _(d=d, m=m):
                value_wait(d, 0, m)
        given = subtract(rest[m], in_buf[0, 0, m], in_buf[1, 0, m])
        for d in range(2):
            second_edge[m][d] = own_gain(d, m, given[:, edge_at[d]])

            @pl.when(patient[d])
            def _(d=d, m=m):
                out_buf[d, 1, m] = second_edge[m][d]

            send(d, value_copy(d, 1, m), patient[d])
        now[m] = inverse(m, given)
        rest[m] = inside(m, now[m])
        for d in range(2):
            ahead(d, 2, m, rest[m])
            send(d, value_copy(d, 2, m), None)
    for m in range(members):
        for d in range(2):
            send(d, gain_copy(d, m), patient[d])

    for m in range(members):
        for d in range(2):
            @pl.when(has[d])
            def _(d=d, m=m):
                value_wait(d, 1, m)

            @pl.when(has[d] & hasty[d])
            def _(d=d, m=m):
                gain_wait(d, m)

            @pl.when(hasty[d])
            def _(d=d, m=m):
                mid_edge[d, m] = in_buf[d, 1, m] - far_gain(d, m, first_edge[m][d])

            @pl.when(patient[d])
            def _(d=d, m=m):
                mid_edge[d, m] = in_buf[d, 1, m]

        given = subtract(rest[m], mid_edge[0, m], mid_edge[1, m])
        for d in range(2):
            last_edge[d, m] = own_gain(d, m, given[:, edge_at[d]])
        now[m] = inverse(m, given)
        rest[m] = inside(m, now[m])
        for d in range(2):
            ahead(d, 3, m, rest[m])
            send(d, value_copy(d, 3, m), None)

    for m in range(members):
        for d in range(2):
            @pl.when(has[d])
            def _(d=d, m=m):
                value_wait(d, 2, m)

            @pl.when(has[d] & patient[d])
            def _(d=d, m=m):
                gain_wait(d, m)

        came_in = [in_buf[d, 2, m] - far_gain(d, m, second_edge[m][d]) for d in range(2)]
        now[m] = inverse(m, subtract(rest[m], *came_in))
        left[m] = inside(m, now[m])

    loads[7].wait()

    def finish(d, total):
        at = d * (planes - 1)
        for m in range(members):
            @pl.when(jnp.where(d == 0, me_c > 0, me_c < ranks - 1))
            def _(m=m):
                value_wait(d, 3, m)

        for m in range(members):
            came_in = in_buf[d, 3, m] - far_gain(d, m, last_edge[d, m])
            value = weighed(lambda w: diag[m, w, :, at].astype(F32), left[m, :, at] - came_in)
            adj[m, :, at] = value
        return gather(at, total)

    def gather(at, total):
        def field(i, total):
            m, u = i // unknowns, i % unknowns
            pieces = split(adj[m, u, at])
            lhs = []
            for value in pieces:
                part_lhs = []
                for y in range(columns):
                    wide = jnp.broadcast_to(value[y : y + 1], (16, layers)).astype(BF16)
                    wide = jnp.concatenate([wide] * (blocks // 16), axis=0)
                    part_lhs.append(mask[at, y] * wide)
                lhs.append(jnp.concatenate(part_lhs, axis=1))
            lhs = jnp.concatenate(lhs, axis=0)
            rhs = sens[i, pl.ds(at * columns, columns)].reshape(columns * layers, sens.shape[-1])
            return total + jnp.dot(lhs, rhs, preferred_element_type=F32)

        if blocks <= 64:
            for i in range(fields):
                total = field(i, total)
            return total
        return lax.fori_loop(0, fields, field, total)

    close = lax.rem(me_c + 1, 2)
    total = jnp.zeros((2 * blocks, sens.shape[-1]), F32)
    total = finish(close, total)
    for x in range(1, planes - 1):
        for m in range(members):
            adj[m, :, x] = weighed(lambda w: diag[m, w, :, x].astype(F32), left[m, :, x])
        total = gather(x, total)
    total = finish(1 - close, total)
    total = total[:blocks] + total[blocks:]
    for c in range(ranks):
        part[c] = total[c * blk_dev : (c + 1) * blk_dev]
    got[me] = part[me_c]

    def part_copy(c, e):
        return pltpu.make_async_remote_copy(
            src_ref=part.at[c], dst_ref=got.at[me], send_sem=part_ssem, recv_sem=part_rsem,
            device_id=(c, e), device_id_type=MESH,
        )

    pl.semaphore_wait(here_sem, len(far))

    def give(to):
        @pl.when(me != to)
        def _():
            part_copy(to // groups, to % groups).start()

    for_each(devices, give)
    others = got.at[pl.ds(0, devices - 1)]
    everything = pltpu.make_async_remote_copy(
        src_ref=others, dst_ref=others, send_sem=part_ssem, recv_sem=part_rsem,
        device_id=next_id, device_id_type=MESH,
    )
    everything.wait_recv()
    got_out[...] = jnp.sum(got[...], axis=0)

    everything.wait_send()
    for d in range(2):
        @pl.when(has[d])
        def _(d=d):
            pltpu.make_async_remote_copy(
                src_ref=out_buf.at[d], dst_ref=out_buf.at[d], send_sem=send_sem.at[d],
                recv_sem=send_sem.at[d], device_id=next_id, device_id_type=MESH,
            ).wait_send()


def write_out(adjoint, gradient, adjoint_hbm, gradient_hbm, sem):
    copies = [
        pltpu.make_async_copy(adjoint, adjoint_hbm, sem.at[0]),
        pltpu.make_async_copy(gradient, gradient_hbm, sem.at[1]),
    ]
    for copy in copies:
        copy.start()
    for copy in copies:
        copy.wait()


def solution(mesh):
    ranks, groups = mesh.shape["cells"], mesh.shape["ens"]
    assert (ranks * groups) & (ranks * groups - 1) == 0

    def body(later_adjoint, coupling, diag_inverse, sensitivity, well_cells, well_misfit, block_map):
        members, unknowns, planes, columns, layers = later_adjoint.shape
        params = sensitivity.shape[-1]
        rows = planes * columns
        blk_dev = 4
        blocks = ranks * blk_dev
        fields = members * unknowns
        sens = sensitivity.reshape(fields, rows, layers, params)
        wells = well_cells.reshape(1, -1)
        edge = (members, unknowns, columns, layers)
        any_spec = pl.BlockSpec(memory_space=pl.ANY)
        vmem_spec = pl.BlockSpec(memory_space=pltpu.VMEM)
        dma = pltpu.SemaphoreType.DMA
        adjoint, gradient = pl.pallas_call(
            functools.partial(kernel, ranks, groups, blocks),
            out_shape=(
                pltpu.VMEM(later_adjoint.shape, F32),
                pltpu.VMEM((blk_dev, params), F32),
            ),
            in_specs=[any_spec] * 7,
            out_specs=(vmem_spec, vmem_spec),
            scratch_shapes=[
                pltpu.VMEM(later_adjoint.shape, F32),
                pltpu.VMEM(coupling.shape, BF16),
                pltpu.VMEM(diag_inverse.shape, BF16),
                pltpu.VMEM(sens.shape, BF16),
                pltpu.VMEM(wells.shape, jnp.int32),
                pltpu.VMEM(well_misfit.shape, F32),
                pltpu.VMEM(block_map.shape, jnp.int32),
                pltpu.VMEM(later_adjoint.shape, F32),
                pltpu.VMEM((2, 4 + unknowns) + edge, F32),
                pltpu.VMEM((2, 4 + unknowns) + edge, F32),
                pltpu.VMEM((2,) + edge, F32),
                pltpu.VMEM((2,) + edge, F32),
                pltpu.VMEM(later_adjoint.shape, F32),
                pltpu.VMEM((planes, columns, blocks, layers), BF16),
                pltpu.VMEM((ranks, blk_dev, params), F32),
                pltpu.VMEM((ranks * groups, blk_dev, params), F32),
                dma((8,)),
                dma((2, 5, members)),
                dma((2,)),
                dma,
                dma,
                pltpu.SemaphoreType.REGULAR,
            ],
            compiler_params=pltpu.CompilerParams(collective_id=0, has_side_effects=True),
        )(later_adjoint, coupling, diag_inverse, sens, wells, well_misfit, block_map)
        return pl.pallas_call(
            write_out,
            out_shape=(
                jax.ShapeDtypeStruct(adjoint.shape, F32),
                jax.ShapeDtypeStruct(gradient.shape, F32),
            ),
            in_specs=[vmem_spec] * 2,
            out_specs=(any_spec, any_spec),
            scratch_shapes=[dma((2,))],
        )(*[pltpu.with_memory_space_constraint(a, pltpu.VMEM) for a in (adjoint, gradient)])

    placed = (
        P("ens", None, "cells", None, None),
        P("ens", None, None, None, "cells", None, None),
        P("ens", None, None, "cells", None, None),
        P("ens", None, "cells", None, None, None),
        P(),
        P("ens", None, None),
        P("cells", None, None),
    )
    return jax.shard_map(
        body,
        mesh=mesh,
        in_specs=placed,
        out_specs=(P("ens", None, "cells", None, None), P("cells", None)),
        check_vma=False,
    )
```

time: 25 us -> 21.9 us (0.88)
  Pallas kernels: 24.2 us -> 21.1 us
    pallas_call x1, Pallas kernels: 23.6 us -> 20.4 us  [body(): pl.pallas_call(functools.partial(kernel, ranks, groups, blocks), out_shap...]
where the time goes in v1:
time: 21.9 us; the launch traced here: 21.7 us
  Pallas kernels  21.1 us (96%)
  between operations  0.64 us (3%)
    pallas_call x1, Pallas kernels, body(): pl.pallas_call(functools.partial(kernel, ranks, groups, blocks), out_shap...  20.4 us
    pallas_call x1, Pallas kernels, body(): pl.pallas_call(write_out, out_shape=(jax.ShapeDtypeStruct(adjoint.shape,...  0.65 us

profile of v1, /device:TPU:0, one launch (start us, length us, event | category | flops | bytes accessed | tf_op | source)
XLA Modules:
  0.0 21.7 jit_solution(103724194172145344)
XLA Ops:
  0.6 20.4 %shard_map.86 = (f32[2,4,2,8,128]{4,3,2,1,0:T(8,128)S(1)}, f32[4,128]{1,0:T(4,128)S(1)}) custom-call(f32[2,4,2,8,128]{4,3,2,1,0:T(8,128)} %later_hbm.1, bf16[2,6,4,4,2,8,128]{6,5,4,3,2,1,0:T(8,128)(2,1)} %coup_hbm.1, bf16[2,4,4,2,8,128]{5,4,3,2,1,0:T(8,128)(2,1)} %diag_hbm.1, bf16[8,16,128,128]{3,2,1,0:T(8,128)(2,1)} %bitcast.2, s32[1,256]{1,0:T(1,128)} %bitcast.3, ...), custom_call_target="tpu_custom_call" | custom-call | tf_op jit(solution)/shard_map/pallas_call | solution.py:444
  21.0 0.7 %shard_map.87 = (f32[2,4,2,8,128]{4,3,2,1,0:T(8,128)}, f32[4,128]{1,0:T(4,128)}) custom-call(f32[2,4,2,8,128]{4,3,2,1,0:T(8,128)S(1)} %get-tuple-element.4.adjoint, f32[4,128]{1,0:T(4,128)S(1)} %get-tuple-element.5.gradient), custom_call_target="tpu_custom_call" | custom-call | tf_op jit(solution)/shard_map/pallas_call | solution.py:478

commit v2 on v1

--- a/solution.py
+++ b/solution.py
@@ -105,7 +105,7 @@
     target = (prev_id, next_id)
     edge_at = (0, planes - 1)
     turn = lax.rem(me_c, 4)
-    patient = (turn == 2, turn == 1)
+    patient = (turn == 0, turn == 3)
     GAIN = 4
 
     def remote(d, src, dst, sem):
@@ -207,9 +207,6 @@
     for m in range(members):
         for d in range(2):
             send(d, value_copy(d, 0, m), None)
-    for m in range(members):
-        for d in range(2):
-            send(d, gain_copy(d, m), hasty[d])
     for who in far:
         pl.semaphore_signal(here_sem, inc=1, device_id=who, device_id_type=MESH)
 
@@ -264,6 +261,10 @@
         for y in range(columns):
             hit = jnp.where(bmap[x, y : y + 1, :] == ids, 1.0, 0.0)
             mask[x, y] = hit.astype(BF16)
+
+    for m in range(members):
+        for d in range(2):
+            send(d, gain_copy(d, m), hasty[d])
 
     first_edge = edge
     second_edge = [[None, None] for _ in range(members)]

time: 21.9 us -> 20.3 us (0.927)
  Pallas kernels: 21.1 us -> 19.5 us
    pallas_call x1, Pallas kernels: 20.4 us -> 18.9 us  [body(): pl.pallas_call(functools.partial(kernel, ranks, groups, blocks), out_shap...]
where the time goes in v2:
time: 20.3 us; the launch traced here: 20.2 us
  Pallas kernels  19.5 us (96%)
  between operations  0.64 us (3%)
    pallas_call x1, Pallas kernels, body(): pl.pallas_call(functools.partial(kernel, ranks, groups, blocks), out_shap...  18.9 us
    pallas_call x1, Pallas kernels, body(): pl.pallas_call(write_out, out_shape=(jax.ShapeDtypeStruct(adjoint.shape,...  0.65 us

profile of v2, /device:TPU:0, one launch (start us, length us, event | category | flops | bytes accessed | tf_op | source)
XLA Modules:
  0.0 20.2 jit_solution(4203201968893370062)
XLA Ops:
  0.6 18.9 %shard_map.86 = (f32[2,4,2,8,128]{4,3,2,1,0:T(8,128)S(1)}, f32[4,128]{1,0:T(4,128)S(1)}) custom-call(f32[2,4,2,8,128]{4,3,2,1,0:T(8,128)} %later_hbm.1, bf16[2,6,4,4,2,8,128]{6,5,4,3,2,1,0:T(8,128)(2,1)} %coup_hbm.1, bf16[2,4,4,2,8,128]{5,4,3,2,1,0:T(8,128)(2,1)} %diag_hbm.1, bf16[8,16,128,128]{3,2,1,0:T(8,128)(2,1)} %bitcast.2, s32[1,256]{1,0:T(1,128)} %bitcast.3, ...), custom_call_target="tpu_custom_call" | custom-call | tf_op jit(solution)/shard_map/pallas_call | solution.py:445
  19.5 0.7 %shard_map.87 = (f32[2,4,2,8,128]{4,3,2,1,0:T(8,128)}, f32[4,128]{1,0:T(4,128)}) custom-call(f32[2,4,2,8,128]{4,3,2,1,0:T(8,128)S(1)} %get-tuple-element.4.adjoint, f32[4,128]{1,0:T(4,128)S(1)} %get-tuple-element.5.gradient), custom_call_target="tpu_custom_call" | custom-call | tf_op jit(solution)/shard_map/pallas_call | solution.py:479

commit v3 on v2

--- a/solution.py
+++ b/solution.py
@@ -8,6 +8,7 @@
 from jax.sharding import PartitionSpec as P
 
 ITERS = 4
+ORDER = (0, 1, 4, 3, 2, 5, 6)
 MESH = pl.DeviceIdType.MESH
 F32 = jnp.float32
 BF16 = jnp.bfloat16
@@ -36,7 +37,7 @@
     adj, got_out,
     later, coup, diag, sens, wells, misfit, bmap, source,
     out_buf, in_buf, mid_edge, last_edge, left, mask, part, got,
-    load_sem, recv_sem, send_sem, part_ssem, part_rsem, here_sem,
+    load_sem, recv_sem, send_sem, part_ssem, part_rsem, here_sem, free_sem,
 ):
     members, unknowns, planes, columns, layers = later.shape
     rows = planes * columns
@@ -59,50 +60,50 @@
             ]
         )
     ]
-    for load in loads[:7]:
-        load.start()
+    for i in ORDER:
+        loads[i].start()
 
     barrier = pltpu.get_barrier_semaphore()
-    block_c = 1
-    while (block_c * groups) ** 2 < devices:
-        block_c *= 2
-    columns_c = ranks // block_c
-
-    def wrap(at, size):
-        return jnp.where(at >= size, at - size, at)
-
-    pos_c = lax.rem(me_c, block_c)
-    base_c = me_c - pos_c
-    near = [
-        (base_c + wrap(pos_c + dc, block_c), wrap(me_e + de, groups))
-        for dc in range(block_c) for de in range(groups) if dc or de
-    ]
-    far = [(wrap(me_c + block_c * s, ranks), me_e) for s in range(1, columns_c)]
-    cross_up = (pos_c == block_c - 1) & (me_c < ranks - 1)
-    cross_down = (pos_c == 0) & (me_c > 0)
+    has = (me_c > 0, me_c < ranks - 1)
     next_id = (jnp.minimum(me_c + 1, ranks - 1), me_e)
     prev_id = (jnp.maximum(me_c - 1, 0), me_e)
+    target = (prev_id, next_id)
+    is_root = me == 0
 
     def greet(who):
         pl.semaphore_signal(barrier, inc=1, device_id=who, device_id_type=MESH)
 
-    for who in near + far:
-        greet(who)
-
-    @pl.when(cross_up)
+    for d in range(2):
+        @pl.when(has[d])
+        def _(d=d):
+            greet(target[d])
+
+    @pl.when(is_root)
     def _():
-        greet(next_id)
-
-    @pl.when(cross_down)
-    def _():
-        greet(prev_id)
+        for_each(devices - 1, lambda i: greet(((i + 1) // groups, (i + 1) % groups)))
 
     def greeted():
-        extra = jnp.where(cross_up, 1, 0) + jnp.where(cross_down, 1, 0)
-        pl.semaphore_wait(barrier, len(near) + len(far) + extra)
-
-    has = (me_c > 0, me_c < ranks - 1)
-    target = (prev_id, next_id)
+        known = [jnp.where(flag, 1, 0) for flag in (has[0], has[1], jnp.logical_not(is_root))]
+        pl.semaphore_wait(barrier, known[0] + known[1] + known[2])
+
+    def report():
+        @pl.when(jnp.logical_not(is_root))
+        def _():
+            pl.semaphore_signal(here_sem, inc=1, device_id=(0, 0), device_id_type=MESH)
+
+    def release():
+        @pl.when(is_root)
+        def _():
+            pl.semaphore_wait(here_sem, devices - 1)
+            for_each(devices - 1, lambda i: pl.semaphore_signal(
+                free_sem, inc=1, device_id=((i + 1) // groups, (i + 1) % groups), device_id_type=MESH,
+            ))
+
+    def released():
+        @pl.when(jnp.logical_not(is_root))
+        def _():
+            pl.semaphore_wait(free_sem, 1)
+
     edge_at = (0, planes - 1)
     turn = lax.rem(me_c, 4)
     patient = (turn == 0, turn == 3)
@@ -207,8 +208,7 @@
     for m in range(members):
         for d in range(2):
             send(d, value_copy(d, 0, m), None)
-    for who in far:
-        pl.semaphore_signal(here_sem, inc=1, device_id=who, device_id_type=MESH)
+    report()
 
     now = [inverse(m, source[m]) for m in range(members)]
 
@@ -318,6 +318,8 @@
             ahead(d, 3, m, rest[m])
             send(d, value_copy(d, 3, m), None)
 
+    release()
+
     for m in range(members):
         for d in range(2):
             @pl.when(has[d])
@@ -334,20 +336,23 @@
 
     loads[7].wait()
 
-    def finish(d, total):
+    def finish(d, total, batch):
         at = d * (planes - 1)
-        for m in range(members):
-            @pl.when(jnp.where(d == 0, me_c > 0, me_c < ranks - 1))
-            def _(m=m):
-                value_wait(d, 3, m)
-
-        for m in range(members):
-            came_in = in_buf[d, 3, m] - far_gain(d, m, last_edge[d, m])
-            value = weighed(lambda w: diag[m, w, :, at].astype(F32), left[m, :, at] - came_in)
-            adj[m, :, at] = value
-        return gather(at, total)
-
-    def gather(at, total):
+        for start in range(0, members, batch):
+            these = range(start, min(start + batch, members))
+            for m in these:
+                @pl.when(jnp.where(d == 0, me_c > 0, me_c < ranks - 1))
+                def _(m=m):
+                    value_wait(d, 3, m)
+
+            for m in these:
+                came_in = in_buf[d, 3, m] - far_gain(d, m, last_edge[d, m])
+                value = weighed(lambda w: diag[m, w, :, at].astype(F32), left[m, :, at] - came_in)
+                adj[m, :, at] = value
+            total = gather(at, total, these)
+        return total
+
+    def gather(at, total, these):
         def field(i, total):
             m, u = i // unknowns, i % unknowns
             pieces = split(adj[m, u, at])
@@ -364,19 +369,19 @@
             return total + jnp.dot(lhs, rhs, preferred_element_type=F32)
 
         if blocks <= 64:
-            for i in range(fields):
+            for i in range(these[0] * unknowns, (these[-1] + 1) * unknowns):
                 total = field(i, total)
             return total
-        return lax.fori_loop(0, fields, field, total)
+        return lax.fori_loop(these[0] * unknowns, (these[-1] + 1) * unknowns, field, total)
 
     close = lax.rem(me_c + 1, 2)
     total = jnp.zeros((2 * blocks, sens.shape[-1]), F32)
-    total = finish(close, total)
+    total = finish(close, total, members)
     for x in range(1, planes - 1):
         for m in range(members):
             adj[m, :, x] = weighed(lambda w: diag[m, w, :, x].astype(F32), left[m, :, x])
-        total = gather(x, total)
-    total = finish(1 - close, total)
+        total = gather(x, total, range(members))
+    total = finish(1 - close, total, 1)
     total = total[:blocks] + total[blocks:]
     for c in range(ranks):
         part[c] = total[c * blk_dev : (c + 1) * blk_dev]
@@ -388,7 +393,7 @@
             device_id=(c, e), device_id_type=MESH,
         )
 
-    pl.semaphore_wait(here_sem, len(far))
+    released()
 
     def give(to):
         @pl.when(me != to)
@@ -473,6 +478,7 @@
                 dma,
                 dma,
                 pltpu.SemaphoreType.REGULAR,
+                pltpu.SemaphoreType.REGULAR,
             ],
             compiler_params=pltpu.CompilerParams(collective_id=0, has_side_effects=True),
         )(later_adjoint, coupling, diag_inverse, sens, wells, well_misfit, block_map)

time: 20.3 us -> 20 us (0.985)
  Pallas kernels: 19.5 us -> 19.2 us
    pallas_call x1, Pallas kernels: 18.9 us -> 18.6 us  [body(): pl.pallas_call(functools.partial(kernel, ranks, groups, blocks), out_shap...]
where the time goes in v3:
time: 20 us; the launch traced here: 19.9 us
  Pallas kernels  19.2 us (96%)
  between operations  0.64 us (3%)
    pallas_call x1, Pallas kernels, body(): pl.pallas_call(functools.partial(kernel, ranks, groups, blocks), out_shap...  18.6 us
    pallas_call x1, Pallas kernels, body(): pl.pallas_call(write_out, out_shape=(jax.ShapeDtypeStruct(adjoint.shape,...  0.65 us

profile of v3, /device:TPU:0, one launch (start us, length us, event | category | flops | bytes accessed | tf_op | source)
XLA Modules:
  0.0 19.9 jit_solution(1264923420551212549)
XLA Ops:
  0.6 18.6 %shard_map.86 = (f32[2,4,2,8,128]{4,3,2,1,0:T(8,128)S(1)}, f32[4,128]{1,0:T(4,128)S(1)}) custom-call(f32[2,4,2,8,128]{4,3,2,1,0:T(8,128)} %later_hbm.1, bf16[2,6,4,4,2,8,128]{6,5,4,3,2,1,0:T(8,128)(2,1)} %coup_hbm.1, bf16[2,4,4,2,8,128]{5,4,3,2,1,0:T(8,128)(2,1)} %diag_hbm.1, bf16[8,16,128,128]{3,2,1,0:T(8,128)(2,1)} %bitcast.2, s32[1,256]{1,0:T(1,128)} %bitcast.3, ...), custom_call_target="tpu_custom_call" | custom-call | tf_op jit(solution)/shard_map/pallas_call | solution.py:450
  19.2 0.7 %shard_map.87 = (f32[2,4,2,8,128]{4,3,2,1,0:T(8,128)}, f32[4,128]{1,0:T(4,128)}) custom-call(f32[2,4,2,8,128]{4,3,2,1,0:T(8,128)S(1)} %get-tuple-element.4.adjoint, f32[4,128]{1,0:T(4,128)S(1)} %get-tuple-element.5.gradient), custom_call_target="tpu_custom_call" | custom-call | tf_op jit(solution)/shard_map/pallas_call | solution.py:485

commit v4 on v3

--- a/solution.py
+++ b/solution.py
@@ -8,22 +8,21 @@
 from jax.sharding import PartitionSpec as P
 
 ITERS = 4
-ORDER = (0, 1, 4, 3, 2, 5, 6)
 MESH = pl.DeviceIdType.MESH
 F32 = jnp.float32
 BF16 = jnp.bfloat16
 
 
-def for_each(count, step):
-    if count <= 64:
-        for i in range(count):
+def for_each(start, stop, step):
+    if stop - start <= 64:
+        for i in range(start, stop):
             step(i)
     else:
         def body(i, carry):
             step(i)
             return carry
 
-        lax.fori_loop(0, count, body, 0)
+        lax.fori_loop(start, stop, body, 0)
 
 
 def split(value):
@@ -36,8 +35,8 @@
     later_hbm, coup_hbm, diag_hbm, sens_hbm, wells_hbm, misfit_hbm, map_hbm,
     adj, got_out,
     later, coup, diag, sens, wells, misfit, bmap, source,
-    out_buf, in_buf, mid_edge, last_edge, left, mask, part, got,
-    load_sem, recv_sem, send_sem, part_ssem, part_rsem, here_sem, free_sem,
+    out_buf, in_buf, mid_edge, last_edge, left, mask, head_mask, part, got,
+    load_sem, recv_sem, send_sem, part_ssem, part_rsem, here_sem,
 ):
     members, unknowns, planes, columns, layers = later.shape
     rows = planes * columns
@@ -45,23 +44,46 @@
     devices = ranks * groups
     blk_dev = blocks // ranks
     fields = members * unknowns
+    head = 2 * blk_dev
     me_c = lax.axis_index("cells")
     me_e = lax.axis_index("ens")
     me = me_c * groups + me_e
-    assert planes >= 2
-
-    loads = [
-        pltpu.make_async_copy(src, dst, load_sem.at[i])
+    assert planes == 2
+
+    close = lax.rem(me_c + 1, 2)
+    open_ = 1 - close
+    here, there = pl.ds(open_, 1), pl.ds(close, 1)
+
+    def load(i, src, dst):
+        return pltpu.make_async_copy(src, dst, load_sem.at[i])
+
+    first_loads = [
+        load(i, src, dst)
         for i, (src, dst) in enumerate(
             [
-                (wells_hbm, wells), (misfit_hbm, misfit), (later_hbm, later), (diag_hbm, diag),
-                (coup_hbm.at[:, 0:2], coup.at[:, 0:2]), (coup_hbm.at[:, 2:6], coup.at[:, 2:6]),
-                (map_hbm, bmap), (sens_hbm, sens),
+                (wells_hbm, wells), (misfit_hbm, misfit),
+                (coup_hbm.at[:, there, :, :, here], coup.at[:, there, :, :, here]),
+                (diag_hbm.at[:, :, :, here], diag.at[:, :, :, here]),
+                (later_hbm.at[:, :, here], later.at[:, :, here]),
             ]
         )
     ]
-    for i in ORDER:
-        loads[i].start()
+    next_loads = [
+        load(i, src, dst)
+        for i, (src, dst) in enumerate(
+            [
+                (coup_hbm.at[:, here], coup.at[:, here]),
+                (coup_hbm.at[:, there, :, :, there], coup.at[:, there, :, :, there]),
+                (coup_hbm.at[:, 2:6], coup.at[:, 2:6]),
+                (diag_hbm.at[:, :, :, there], diag.at[:, :, :, there]),
+                (later_hbm.at[:, :, there], later.at[:, :, there]),
+            ]
+        )
+    ]
+    map_load = load(0, map_hbm, bmap)
+    sens_load = load(1, sens_hbm, sens)
+    for copy in first_loads:
+        copy.start()
 
     barrier = pltpu.get_barrier_semaphore()
     has = (me_c > 0, me_c < ranks - 1)
@@ -80,7 +102,7 @@
 
     @pl.when(is_root)
     def _():
-        for_each(devices - 1, lambda i: greet(((i + 1) // groups, (i + 1) % groups)))
+        for_each(1, devices, lambda i: greet((i // groups, i % groups)))
 
     def greeted():
         known = [jnp.where(flag, 1, 0) for flag in (has[0], has[1], jnp.logical_not(is_root))]
@@ -95,14 +117,14 @@
         @pl.when(is_root)
         def _():
             pl.semaphore_wait(here_sem, devices - 1)
-            for_each(devices - 1, lambda i: pl.semaphore_signal(
-                free_sem, inc=1, device_id=((i + 1) // groups, (i + 1) % groups), device_id_type=MESH,
+            for_each(1, devices, lambda i: pl.semaphore_signal(
+                here_sem, inc=1, device_id=(i // groups, i % groups), device_id_type=MESH,
             ))
 
     def released():
         @pl.when(jnp.logical_not(is_root))
         def _():
-            pl.semaphore_wait(free_sem, 1)
+            pl.semaphore_wait(here_sem, 1)
 
     edge_at = (0, planes - 1)
     turn = lax.rem(me_c, 4)
@@ -140,11 +162,13 @@
         def _(d=d):
             in_buf[d] = jnp.zeros(in_buf.shape[1:], F32)
 
-    loads[0].wait()
-    loads[1].wait()
+    first_loads[0].wait()
+    first_loads[1].wait()
     total_wells = wells.shape[1]
     rel = wells[...] - me_c * count
-    row_lo = lax.broadcasted_iota(jnp.int32, (rows, total_wells), 0) * layers
+    row = lax.broadcasted_iota(jnp.int32, (rows, total_wells), 0)
+    row = row + open_ * columns
+    row_lo = jnp.where(row >= rows, row - rows, row) * layers
     in_row = (rel >= row_lo) & (rel < row_lo + layers)
     lane = wells[...] & (layers - 1)
     at_lane = lax.broadcasted_iota(jnp.int32, (layers, total_wells), 0) == lane
@@ -163,8 +187,7 @@
             jnp.concatenate(piece, axis=0), at_lane, (((1,), (1,)), ((), ())),
             preferred_element_type=F32,
         )
-    loads[2].wait()
-    source[...] = later[...] + injected.reshape(later.shape)
+    injected = injected.reshape(members, unknowns, planes, columns, layers)
 
     def weighed(weights, values):
         out = None
@@ -176,27 +199,29 @@
     def inverse(m, rhs):
         return weighed(lambda w: diag[m, w].astype(F32), rhs)
 
-    loads[3].wait()
-    loads[4].wait()
-
     def own_gain(d, m, values):
         return weighed(lambda w: out_buf[d, GAIN + w, m], values)
 
     def far_gain(d, m, values):
         return weighed(lambda w: in_buf[d, GAIN + w, m], values)
 
-    for m in range(members):
-        for d in range(2):
-            at = edge_at[d]
+    def set_edge(d, place):
+        for m in range(members):
             for w in range(unknowns):
                 out_buf[d, GAIN + w, m] = weighed(
-                    lambda u: coup[m, 1 - d, u, :, at].astype(F32), diag[m, w, :, at].astype(F32)
+                    lambda u: coup[m, 1 - d, u, :, d].astype(F32), diag[m, w, :, d].astype(F32)
                 )
-    edge = [[None, None] for _ in range(members)]
-    for m in range(members):
-        for d in range(2):
-            edge[m][d] = own_gain(d, m, source[m, :, edge_at[d]])
-            out_buf[d, 0, m] = edge[m][d]
+        for m in range(members):
+            value = later[m, :, d] + injected[m, :, place]
+            source[m, :, d] = value
+            out_buf[d, 0, m] = own_gain(d, m, value)
+
+    first_loads[2].wait()
+    first_loads[3].wait()
+    first_loads[4].wait()
+    for copy in next_loads:
+        copy.start()
+    set_edge(open_, 0)
     greeted()
 
     def send(d, copy, when):
@@ -205,9 +230,31 @@
             copy.start()
 
     hasty = tuple(jnp.logical_not(p) for p in patient)
-    for m in range(members):
-        for d in range(2):
-            send(d, value_copy(d, 0, m), None)
+    slow = (open_ == 0, open_ == 1)
+    side = jnp.where(open_ == 1, me_c + 1, me_c - 1)
+    side = jnp.clip(side, 0, ranks - 1)
+    has_side = jnp.where(open_ == 1, me_c < ranks - 1, me_c > 0)
+
+    @pl.when(has_side)
+    def _():
+        for m in range(members):
+            pltpu.make_async_remote_copy(
+                src_ref=out_buf.at[open_, 0, m], dst_ref=in_buf.at[close, 0, m],
+                send_sem=send_sem.at[open_], recv_sem=recv_sem.at[close, 0, m],
+                device_id=(side, me_e), device_id_type=MESH,
+            ).start()
+
+    for d in range(2):
+        for m in range(members):
+            send(d, gain_copy(d, m), hasty[d] & slow[d])
+
+    for copy in next_loads:
+        copy.wait()
+    map_load.start()
+    set_edge(close, 1)
+    for d in range(2):
+        for m in range(members):
+            send(d, value_copy(d, 0, m), jnp.logical_not(slow[d]))
     report()
 
     now = [inverse(m, source[m]) for m in range(members)]
@@ -244,8 +291,7 @@
             [first_plane[:, None], rest[:, 1 : planes - 1], last_plane[:, None]], axis=1
         ) if planes > 2 else jnp.stack([first_plane, last_plane], axis=1)
 
-    loads[5].wait()
-    loads[7].start()
+    sens_load.start()
     rest = [inside(m, now[m]) for m in range(members)]
     for m in range(members):
         for d in range(2):
@@ -255,18 +301,21 @@
 
             send(d, value_copy(d, 1, m), hasty[d])
 
-    loads[6].wait()
+    map_load.wait()
     ids = lax.broadcasted_iota(jnp.int32, (blocks, layers), 0)
+    head_ids = lax.broadcasted_iota(jnp.int32, (2 * head, layers), 0)
+    head_ids = jnp.where(head_ids >= head, head_ids - head, head_ids)
     for x in range(planes):
         for y in range(columns):
             hit = jnp.where(bmap[x, y : y + 1, :] == ids, 1.0, 0.0)
             mask[x, y] = hit.astype(BF16)
-
-    for m in range(members):
-        for d in range(2):
-            send(d, gain_copy(d, m), hasty[d])
-
-    first_edge = edge
+            hit = jnp.where(bmap[x, y : y + 1, :] == head_ids, 1.0, 0.0)
+            head_mask[x, y] = hit.astype(BF16)
+
+    for m in range(members):
+        for d in range(2):
+            send(d, gain_copy(d, m), jnp.logical_not(slow[d]))
+
     second_edge = [[None, None] for _ in range(members)]
     for m in range(members):
         for d in range(2):
@@ -303,7 +352,7 @@
 
             @pl.when(hasty[d])
             def _(d=d, m=m):
-                mid_edge[d, m] = in_buf[d, 1, m] - far_gain(d, m, first_edge[m][d])
+                mid_edge[d, m] = in_buf[d, 1, m] - far_gain(d, m, out_buf[d, 0, m])
 
             @pl.when(patient[d])
             def _(d=d, m=m):
@@ -334,58 +383,61 @@
         now[m] = inverse(m, subtract(rest[m], *came_in))
         left[m] = inside(m, now[m])
 
-    loads[7].wait()
-
-    def finish(d, total, batch):
-        at = d * (planes - 1)
-        for start in range(0, members, batch):
-            these = range(start, min(start + batch, members))
-            for m in these:
-                @pl.when(jnp.where(d == 0, me_c > 0, me_c < ranks - 1))
-                def _(m=m):
-                    value_wait(d, 3, m)
-
-            for m in these:
-                came_in = in_buf[d, 3, m] - far_gain(d, m, last_edge[d, m])
-                value = weighed(lambda w: diag[m, w, :, at].astype(F32), left[m, :, at] - came_in)
-                adj[m, :, at] = value
-            total = gather(at, total, these)
-        return total
-
-    def gather(at, total, these):
+    sens_load.wait()
+
+    def settle(d, these):
+        for m in these:
+            @pl.when(jnp.where(d == 0, me_c > 0, me_c < ranks - 1))
+            def _(m=m):
+                value_wait(d, 3, m)
+
+        for m in these:
+            came_in = in_buf[d, 3, m] - far_gain(d, m, last_edge[d, m])
+            value = weighed(lambda w: diag[m, w, :, d].astype(F32), left[m, :, d] - came_in)
+            adj[m, :, d] = value
+
+    def gather(at, total, these, spread):
         def field(i, total):
-            m, u = i // unknowns, i % unknowns
-            pieces = split(adj[m, u, at])
-            lhs = []
-            for value in pieces:
-                part_lhs = []
-                for y in range(columns):
-                    wide = jnp.broadcast_to(value[y : y + 1], (16, layers)).astype(BF16)
-                    wide = jnp.concatenate([wide] * (blocks // 16), axis=0)
-                    part_lhs.append(mask[at, y] * wide)
-                lhs.append(jnp.concatenate(part_lhs, axis=1))
-            lhs = jnp.concatenate(lhs, axis=0)
+            pieces = split(adj[i // unknowns, i % unknowns, at])
             rhs = sens[i, pl.ds(at * columns, columns)].reshape(columns * layers, sens.shape[-1])
-            return total + jnp.dot(lhs, rhs, preferred_element_type=F32)
-
+            return total + jnp.dot(spread(at, pieces), rhs, preferred_element_type=F32)
+
+        bounds = these[0] * unknowns, (these[-1] + 1) * unknowns
         if blocks <= 64:
-            for i in range(these[0] * unknowns, (these[-1] + 1) * unknowns):
+            for i in range(*bounds):
                 total = field(i, total)
             return total
-        return lax.fori_loop(these[0] * unknowns, (these[-1] + 1) * unknowns, field, total)
-
-    close = lax.rem(me_c + 1, 2)
-    total = jnp.zeros((2 * blocks, sens.shape[-1]), F32)
-    total = finish(close, total, members)
-    for x in range(1, planes - 1):
-        for m in range(members):
-            adj[m, :, x] = weighed(lambda w: diag[m, w, :, x].astype(F32), left[m, :, x])
-        total = gather(x, total, range(members))
-    total = finish(1 - close, total, 1)
-    total = total[:blocks] + total[blocks:]
-    for c in range(ranks):
-        part[c] = total[c * blk_dev : (c + 1) * blk_dev]
-    got[me] = part[me_c]
+        return lax.fori_loop(*bounds, field, total)
+
+    def spread_all(at, pieces):
+        lhs = []
+        for value in pieces:
+            row = []
+            for y in range(columns):
+                wide = jnp.broadcast_to(value[y : y + 1], (16, layers)).astype(BF16)
+                wide = jnp.concatenate([wide] * (blocks // 16), axis=0)
+                row.append(mask[at, y] * wide)
+            lhs.append(jnp.concatenate(row, axis=1))
+        return jnp.concatenate(lhs, axis=0)
+
+    def spread_head(at, pieces):
+        row = []
+        for y in range(columns):
+            wide = [jnp.broadcast_to(value[y : y + 1], (head, layers)) for value in pieces]
+            row.append(head_mask[at, y] * jnp.concatenate(wide, axis=0).astype(BF16))
+        return jnp.concatenate(row, axis=1)
+
+    everyone = range(members)
+    params = sens.shape[-1]
+    settle(close, everyone)
+    total = gather(close, jnp.zeros((2 * blocks, params), F32), everyone, spread_all)
+    top = jnp.zeros((2 * head, params), F32)
+    for m in everyone:
+        settle(open_, [m])
+        top = gather(open_, top, [m], spread_head)
+    top = top[:head] + top[head:] + total[:head] + total[blocks : blocks + head]
+    for c in range(2):
+        part[c] = top[c * blk_dev : (c + 1) * blk_dev]
 
     def part_copy(c, e):
         return pltpu.make_async_remote_copy(
@@ -400,7 +452,13 @@
         def _():
             part_copy(to // groups, to % groups).start()
 
-    for_each(devices, give)
+    for_each(0, 2 * groups, give)
+    total = gather(open_, total, everyone, spread_all)
+    total = total[:blocks] + total[blocks:]
+    for c in range(2, ranks):
+        part[c] = total[c * blk_dev : (c + 1) * blk_dev]
+    got[me] = part[me_c]
+    for_each(2 * groups, devices, give)
     others = got.at[pl.ds(0, devices - 1)]
     everything = pltpu.make_async_remote_copy(
         src_ref=others, dst_ref=others, send_sem=part_ssem, recv_sem=part_rsem,
@@ -470,14 +528,14 @@
                 pltpu.VMEM((2,) + edge, F32),
                 pltpu.VMEM(later_adjoint.shape, F32),
                 pltpu.VMEM((planes, columns, blocks, layers), BF16),
+                pltpu.VMEM((planes, columns, 4 * blk_dev, layers), BF16),
                 pltpu.VMEM((ranks, blk_dev, params), F32),
                 pltpu.VMEM((ranks * groups, blk_dev, params), F32),
-                dma((8,)),
+                dma((5,)),
                 dma((2, 5, members)),
                 dma((2,)),
                 dma,
                 dma,
-                pltpu.SemaphoreType.REGULAR,
                 pltpu.SemaphoreType.REGULAR,
             ],
             compiler_params=pltpu.CompilerParams(collective_id=0, has_side_effects=True),

time: 20 us -> 19.8 us (0.990)
  Pallas kernels: 19.2 us -> 18.9 us
    pallas_call x1, Pallas kernels: 18.6 us -> 18.3 us  [body(): pl.pallas_call(functools.partial(kernel, ranks, groups, blocks), out_shap...]
where the time goes in v4:
time: 19.8 us; the launch traced here: 19.6 us
  Pallas kernels  18.9 us (95%)
  between operations  0.64 us (3%)
    pallas_call x1, Pallas kernels, body(): pl.pallas_call(functools.partial(kernel, ranks, groups, blocks), out_shap...  18.3 us
    pallas_call x1, Pallas kernels, body(): pl.pallas_call(write_out, out_shape=(jax.ShapeDtypeStruct(adjoint.shape,...  0.65 us

profile of v4, /device:TPU:0, one launch (start us, length us, event | category | flops | bytes accessed | tf_op | source)
XLA Modules:
  0.0 19.6 jit_solution(3114221228923914019)
XLA Ops:
  0.6 18.3 %shard_map.86 = (f32[2,4,2,8,128]{4,3,2,1,0:T(8,128)S(1)}, f32[4,128]{1,0:T(4,128)S(1)}) custom-call(f32[2,4,2,8,128]{4,3,2,1,0:T(8,128)} %later_hbm.1, bf16[2,6,4,4,2,8,128]{6,5,4,3,2,1,0:T(8,128)(2,1)} %coup_hbm.1, bf16[2,4,4,2,8,128]{5,4,3,2,1,0:T(8,128)(2,1)} %diag_hbm.1, bf16[8,16,128,128]{3,2,1,0:T(8,128)(2,1)} %bitcast.2, s32[1,256]{1,0:T(1,128)} %bitcast.3, ...), custom_call_target="tpu_custom_call" | custom-call | tf_op jit(solution)/shard_map/pallas_call | solution.py:508
  18.9 0.7 %shard_map.87 = (f32[2,4,2,8,128]{4,3,2,1,0:T(8,128)}, f32[4,128]{1,0:T(4,128)}) custom-call(f32[2,4,2,8,128]{4,3,2,1,0:T(8,128)S(1)} %get-tuple-element.4.adjoint, f32[4,128]{1,0:T(4,128)S(1)} %get-tuple-element.5.gradient), custom_call_target="tpu_custom_call" | custom-call | tf_op jit(solution)/shard_map/pallas_call | solution.py:543

commit v5 on v4

--- a/solution.py
+++ b/solution.py
@@ -35,7 +35,7 @@
     later_hbm, coup_hbm, diag_hbm, sens_hbm, wells_hbm, misfit_hbm, map_hbm,
     adj, got_out,
     later, coup, diag, sens, wells, misfit, bmap, source,
-    out_buf, in_buf, mid_edge, last_edge, left, mask, head_mask, part, got,
+    out_buf, in_buf, mid_edge, last_edge, left, current, mask, head_mask, part, got,
     load_sem, recv_sem, send_sem, part_ssem, part_rsem, here_sem,
 ):
     members, unknowns, planes, columns, layers = later.shape
@@ -82,9 +82,6 @@
     ]
     map_load = load(0, map_hbm, bmap)
     sens_load = load(1, sens_hbm, sens)
-    for copy in first_loads:
-        copy.start()
-
     barrier = pltpu.get_barrier_semaphore()
     has = (me_c > 0, me_c < ranks - 1)
     next_id = (jnp.minimum(me_c + 1, ranks - 1), me_e)
@@ -99,6 +96,9 @@
         @pl.when(has[d])
         def _(d=d):
             greet(target[d])
+
+    for copy in first_loads:
+        copy.start()
 
     @pl.when(is_root)
     def _():
@@ -138,7 +138,8 @@
         )
 
     def value_copy(d, slot, m):
-        return remote(d, out_buf.at[d, slot, m], in_buf.at[1 - d, slot, m], recv_sem.at[1 - d, slot, m])
+        sem = recv_sem.at[1 - d, slot, 0 if slot == 2 else m]
+        return remote(d, out_buf.at[d, slot, m], in_buf.at[1 - d, slot, m], sem)
 
     def gain_copy(d, m):
         both = pl.ds(GAIN, unknowns)
@@ -148,6 +149,12 @@
         pltpu.make_async_remote_copy(
             src_ref=out_buf.at[d, slot, m], dst_ref=in_buf.at[d, slot, m], send_sem=send_sem.at[d],
             recv_sem=recv_sem.at[d, slot, m], device_id=next_id, device_id_type=MESH,
+        ).wait_recv()
+
+    def both_wait(d, slot):
+        pltpu.make_async_remote_copy(
+            src_ref=out_buf.at[d, slot], dst_ref=in_buf.at[d, slot], send_sem=send_sem.at[d],
+            recv_sem=recv_sem.at[d, slot, 0], device_id=next_id, device_id_type=MESH,
         ).wait_recv()
 
     def gain_wait(d, m):
@@ -173,12 +180,12 @@
     lane = wells[...] & (layers - 1)
     at_lane = lax.broadcasted_iota(jnp.int32, (layers, total_wells), 0) == lane
     at_lane = jnp.where(at_lane, 1.0, 0.0).astype(BF16)
-    parts = [[], [], []]
+    parts = [[], []]
     for m in range(members):
         for u in range(unknowns):
             rest = jnp.broadcast_to(misfit[m, u : u + 1, :], (rows, total_wells))
             rest = jnp.where(in_row, rest, 0.0)
-            for i in range(3):
+            for i in range(2):
                 high, rest = split(rest)
                 parts[i].append(high.astype(BF16))
     injected = jnp.zeros((fields * rows, layers), F32)
@@ -223,6 +230,7 @@
         copy.start()
     set_edge(open_, 0)
     greeted()
+    report()
 
     def send(d, copy, when):
         @pl.when(has[d] & when if when is not None else has[d])
@@ -231,18 +239,22 @@
 
     hasty = tuple(jnp.logical_not(p) for p in patient)
     slow = (open_ == 0, open_ == 1)
+    patient_here = (turn == 0) | (turn == 3)
     side = jnp.where(open_ == 1, me_c + 1, me_c - 1)
     side = jnp.clip(side, 0, ranks - 1)
     has_side = jnp.where(open_ == 1, me_c < ranks - 1, me_c > 0)
 
+    def side_copy(slot, m):
+        return pltpu.make_async_remote_copy(
+            src_ref=out_buf.at[open_, slot, m], dst_ref=in_buf.at[close, slot, m],
+            send_sem=send_sem.at[open_], recv_sem=recv_sem.at[close, slot, m],
+            device_id=(side, me_e), device_id_type=MESH,
+        )
+
     @pl.when(has_side)
     def _():
         for m in range(members):
-            pltpu.make_async_remote_copy(
-                src_ref=out_buf.at[open_, 0, m], dst_ref=in_buf.at[close, 0, m],
-                send_sem=send_sem.at[open_], recv_sem=recv_sem.at[close, 0, m],
-                device_id=(side, me_e), device_id_type=MESH,
-            ).start()
+            side_copy(0, m).start()
 
     for d in range(2):
         for m in range(members):
@@ -255,7 +267,6 @@
     for d in range(2):
         for m in range(members):
             send(d, value_copy(d, 0, m), jnp.logical_not(slow[d]))
-    report()
 
     now = [inverse(m, source[m]) for m in range(members)]
 
@@ -294,6 +305,8 @@
     sens_load.start()
     rest = [inside(m, now[m]) for m in range(members)]
     for m in range(members):
+        left[m] = rest[m]
+    for m in range(members):
         for d in range(2):
             @pl.when(hasty[d])
             def _(d=d, m=m):
@@ -318,27 +331,49 @@
 
     second_edge = [[None, None] for _ in range(members)]
     for m in range(members):
-        for d in range(2):
-            @pl.when(has[d])
+        @pl.when(has_side)
+        def _(m=m):
+            value_wait(open_, 0, m)
+
+        @pl.when(has_side & patient_here)
+        def _(m=m):
+            out_buf[open_, 1, m] = own_gain(open_, m, left[m, :, open_] - in_buf[open_, 0, m])
+            side_copy(1, m).start()
+
+        for d in range(2):
+            @pl.when(has[d] & jnp.logical_not(slow[d]))
             def _(d=d, m=m):
                 value_wait(d, 0, m)
+
         given = subtract(rest[m], in_buf[0, 0, m], in_buf[1, 0, m])
         for d in range(2):
             second_edge[m][d] = own_gain(d, m, given[:, edge_at[d]])
-
-            @pl.when(patient[d])
-            def _(d=d, m=m):
-                out_buf[d, 1, m] = second_edge[m][d]
-
-            send(d, value_copy(d, 1, m), patient[d])
         now[m] = inverse(m, given)
         rest[m] = inside(m, now[m])
         for d in range(2):
             ahead(d, 2, m, rest[m])
+    for m in range(members):
+        for d in range(2):
             send(d, value_copy(d, 2, m), None)
     for m in range(members):
         for d in range(2):
             send(d, gain_copy(d, m), patient[d])
+
+    def inside_plane(m, d):
+        def coupled(k, plane, value):
+            return weighed(lambda u: coup[m, k, u, :, plane].astype(F32), value)
+
+        value = current[m, :, d]
+        moved = pltpu.roll(coupled(2, d, value), 1, 1)
+        total = jnp.where(col_at[:, 0] == 0, 0.0, moved)
+        moved = pltpu.roll(coupled(3, d, value), columns - 1, 1)
+        total = total + jnp.where(col_at[:, 0] == columns - 1, 0.0, moved)
+        moved = pltpu.roll(coupled(4, d, value), 1, 2)
+        total = total + jnp.where(lane_at[:, 0] == 0, 0.0, moved)
+        moved = pltpu.roll(coupled(5, d, value), layers - 1, 2)
+        total = total + jnp.where(lane_at[:, 0] == layers - 1, 0.0, moved)
+        total = total + coupled(1 - d, 1 - d, current[m, :, 1 - d])
+        return source[m, :, d] - total
 
     for m in range(members):
         for d in range(2):
@@ -359,29 +394,41 @@
                 mid_edge[d, m] = in_buf[d, 1, m]
 
         given = subtract(rest[m], mid_edge[0, m], mid_edge[1, m])
+        current[m] = inverse(m, given)
         for d in range(2):
             last_edge[d, m] = own_gain(d, m, given[:, edge_at[d]])
-        now[m] = inverse(m, given)
-        rest[m] = inside(m, now[m])
-        for d in range(2):
-            ahead(d, 3, m, rest[m])
-            send(d, value_copy(d, 3, m), None)
+        value = inside_plane(m, open_)
+        left[m, :, open_] = value
+        out_buf[open_, 3, m] = own_gain(open_, m, value)
+
+        @pl.when(has_side)
+        def _(m=m):
+            side_copy(3, m).start()
+
+    for m in range(members):
+        value = inside_plane(m, close)
+        left[m, :, close] = value
+        out_buf[close, 3, m] = own_gain(close, m, value)
+        for d in range(2):
+            send(d, value_copy(d, 3, m), jnp.logical_not(slow[d]))
 
     release()
 
-    for m in range(members):
-        for d in range(2):
-            @pl.when(has[d])
-            def _(d=d, m=m):
-                value_wait(d, 2, m)
-
+    for d in range(2):
+        @pl.when(has[d])
+        def _(d=d):
+            both_wait(d, 2)
+
+    for m in range(members):
+        for d in range(2):
             @pl.when(has[d] & patient[d])
             def _(d=d, m=m):
                 gain_wait(d, m)
 
         came_in = [in_buf[d, 2, m] - far_gain(d, m, second_edge[m][d]) for d in range(2)]
-        now[m] = inverse(m, subtract(rest[m], *came_in))
-        left[m] = inside(m, now[m])
+        current[m] = inverse(m, subtract(left[m], *came_in))
+        for d in range(2):
+            left[m, :, d] = inside_plane(m, d) + far_gain(d, m, last_edge[d, m])
 
     sens_load.wait()
 
@@ -392,8 +439,8 @@
                 value_wait(d, 3, m)
 
         for m in these:
-            came_in = in_buf[d, 3, m] - far_gain(d, m, last_edge[d, m])
-            value = weighed(lambda w: diag[m, w, :, d].astype(F32), left[m, :, d] - came_in)
+            given = left[m, :, d] - in_buf[d, 3, m]
+            value = weighed(lambda w: diag[m, w, :, d].astype(F32), given)
             adj[m, :, d] = value
 
     def gather(at, total, these, spread):
@@ -527,6 +574,7 @@
                 pltpu.VMEM((2,) + edge, F32),
                 pltpu.VMEM((2,) + edge, F32),
                 pltpu.VMEM(later_adjoint.shape, F32),
+                pltpu.VMEM(later_adjoint.shape, F32),
                 pltpu.VMEM((planes, columns, blocks, layers), BF16),
                 pltpu.VMEM((planes, columns, 4 * blk_dev, layers), BF16),
                 pltpu.VMEM((ranks, blk_dev, params), F32),

time: 19.8 us -> 19.7 us (level)
  no operation moved by 1% of the time
where the time goes in v5:
time: 19.7 us; the launch traced here: 19.5 us
  Pallas kernels  18.8 us (95%)
  between operations  0.64 us (3%)
    pallas_call x1, Pallas kernels, body(): pl.pallas_call(functools.partial(kernel, ranks, groups, blocks), out_shap...  18.2 us
    pallas_call x1, Pallas kernels, body(): pl.pallas_call(write_out, out_shape=(jax.ShapeDtypeStruct(adjoint.shape,...  0.65 us

profile of v5, /device:TPU:0, one launch (start us, length us, event | category | flops | bytes accessed | tf_op | source)
XLA Modules:
  0.0 19.5 jit_solution(3179952694256125253)
XLA Ops:
  0.6 18.2 %shard_map.86 = (f32[2,4,2,8,128]{4,3,2,1,0:T(8,128)S(1)}, f32[4,128]{1,0:T(4,128)S(1)}) custom-call(f32[2,4,2,8,128]{4,3,2,1,0:T(8,128)} %later_hbm.1, bf16[2,6,4,4,2,8,128]{6,5,4,3,2,1,0:T(8,128)(2,1)} %coup_hbm.1, bf16[2,4,4,2,8,128]{5,4,3,2,1,0:T(8,128)(2,1)} %diag_hbm.1, bf16[8,16,128,128]{3,2,1,0:T(8,128)(2,1)} %bitcast.2, s32[1,256]{1,0:T(1,128)} %bitcast.3, ...), custom_call_target="tpu_custom_call" | custom-call | tf_op jit(solution)/shard_map/pallas_call | solution.py:555
  18.8 0.7 %shard_map.87 = (f32[2,4,2,8,128]{4,3,2,1,0:T(8,128)}, f32[4,128]{1,0:T(4,128)}) custom-call(f32[2,4,2,8,128]{4,3,2,1,0:T(8,128)S(1)} %get-tuple-element.4.adjoint, f32[4,128]{1,0:T(4,128)S(1)} %get-tuple-element.5.gradient), custom_call_target="tpu_custom_call" | custom-call | tf_op jit(solution)/shard_map/pallas_call | solution.py:591

commit v6 on v5

--- a/solution.py
+++ b/solution.py
@@ -36,7 +36,7 @@
     adj, got_out,
     later, coup, diag, sens, wells, misfit, bmap, source,
     out_buf, in_buf, mid_edge, last_edge, left, current, mask, head_mask, part, got,
-    load_sem, recv_sem, send_sem, part_ssem, part_rsem, here_sem,
+    load_sem, recv_sem, send_sem, part_rsem, here_sem,
 ):
     members, unknowns, planes, columns, layers = later.shape
     rows = planes * columns
@@ -137,31 +137,34 @@
             device_id=target[d], device_id_type=MESH,
         )
 
+    def place(slot, m):
+        return 0 if slot == 2 else 1 + {0: 0, 1: 1, 3: 2, GAIN: 3}[slot] * members + m
+
     def value_copy(d, slot, m):
-        sem = recv_sem.at[1 - d, slot, 0 if slot == 2 else m]
+        sem = recv_sem.at[1 - d, place(slot, m)]
         return remote(d, out_buf.at[d, slot, m], in_buf.at[1 - d, slot, m], sem)
 
     def gain_copy(d, m):
         both = pl.ds(GAIN, unknowns)
-        return remote(d, out_buf.at[d, both, m], in_buf.at[1 - d, both, m], recv_sem.at[1 - d, GAIN, m])
+        return remote(d, out_buf.at[d, both, m], in_buf.at[1 - d, both, m], recv_sem.at[1 - d, place(GAIN, m)])
 
     def value_wait(d, slot, m):
         pltpu.make_async_remote_copy(
             src_ref=out_buf.at[d, slot, m], dst_ref=in_buf.at[d, slot, m], send_sem=send_sem.at[d],
-            recv_sem=recv_sem.at[d, slot, m], device_id=next_id, device_id_type=MESH,
+            recv_sem=recv_sem.at[d, place(slot, m)], device_id=next_id, device_id_type=MESH,
         ).wait_recv()
 
     def both_wait(d, slot):
         pltpu.make_async_remote_copy(
             src_ref=out_buf.at[d, slot], dst_ref=in_buf.at[d, slot], send_sem=send_sem.at[d],
-            recv_sem=recv_sem.at[d, slot, 0], device_id=next_id, device_id_type=MESH,
+            recv_sem=recv_sem.at[d, place(slot, 0)], device_id=next_id, device_id_type=MESH,
         ).wait_recv()
 
     def gain_wait(d, m):
         both = pl.ds(GAIN, unknowns)
         pltpu.make_async_remote_copy(
             src_ref=out_buf.at[d, both, m], dst_ref=in_buf.at[d, both, m], send_sem=send_sem.at[d],
-            recv_sem=recv_sem.at[d, GAIN, m], device_id=next_id, device_id_type=MESH,
+            recv_sem=recv_sem.at[d, place(GAIN, m)], device_id=next_id, device_id_type=MESH,
         ).wait_recv()
 
     for d in range(2):
@@ -247,7 +250,7 @@
     def side_copy(slot, m):
         return pltpu.make_async_remote_copy(
             src_ref=out_buf.at[open_, slot, m], dst_ref=in_buf.at[close, slot, m],
-            send_sem=send_sem.at[open_], recv_sem=recv_sem.at[close, slot, m],
+            send_sem=send_sem.at[open_], recv_sem=recv_sem.at[close, place(slot, m)],
             device_id=(side, me_e), device_id_type=MESH,
         )
 
@@ -488,7 +491,7 @@
 
     def part_copy(c, e):
         return pltpu.make_async_remote_copy(
-            src_ref=part.at[c], dst_ref=got.at[me], send_sem=part_ssem, recv_sem=part_rsem,
+            src_ref=part.at[c], dst_ref=got.at[me], send_sem=load_sem.at[0], recv_sem=part_rsem,
             device_id=(c, e), device_id_type=MESH,
         )
 
@@ -508,7 +511,7 @@
     for_each(2 * groups, devices, give)
     others = got.at[pl.ds(0, devices - 1)]
     everything = pltpu.make_async_remote_copy(
-        src_ref=others, dst_ref=others, send_sem=part_ssem, recv_sem=part_rsem,
+        src_ref=others, dst_ref=others, send_sem=load_sem.at[0], recv_sem=part_rsem,
         device_id=next_id, device_id_type=MESH,
     )
     everything.wait_recv()
@@ -580,9 +583,8 @@
                 pltpu.VMEM((ranks, blk_dev, params), F32),
                 pltpu.VMEM((ranks * groups, blk_dev, params), F32),
                 dma((5,)),
-                dma((2, 5, members)),
+                dma((2, 1 + 4 * members)),
                 dma((2,)),
-                dma,
                 dma,
                 pltpu.SemaphoreType.REGULAR,
             ],

time: 19.7 us -> 19.7 us (level)
  no operation moved by 1% of the time
where the time goes in v6:
time: 19.7 us; the launch traced here: 19.4 us
  Pallas kernels  18.8 us (95%)
  between operations  0.64 us (3%)
    pallas_call x1, Pallas kernels, body(): pl.pallas_call(functools.partial(kernel, ranks, groups, blocks), out_shap...  18.1 us
    pallas_call x1, Pallas kernels, body(): pl.pallas_call(write_out, out_shape=(jax.ShapeDtypeStruct(adjoint.shape,...  0.65 us

profile of v6, /device:TPU:0, one launch (start us, length us, event | category | flops | bytes accessed | tf_op | source)
XLA Modules:
  0.0 19.4 jit_solution(2723070288900595385)
XLA Ops:
  0.6 18.1 %shard_map.86 = (f32[2,4,2,8,128]{4,3,2,1,0:T(8,128)S(1)}, f32[4,128]{1,0:T(4,128)S(1)}) custom-call(f32[2,4,2,8,128]{4,3,2,1,0:T(8,128)} %later_hbm.1, bf16[2,6,4,4,2,8,128]{6,5,4,3,2,1,0:T(8,128)(2,1)} %coup_hbm.1, bf16[2,4,4,2,8,128]{5,4,3,2,1,0:T(8,128)(2,1)} %diag_hbm.1, bf16[8,16,128,128]{3,2,1,0:T(8,128)(2,1)} %bitcast.2, s32[1,256]{1,0:T(1,128)} %bitcast.3, ...), custom_call_target="tpu_custom_call" | custom-call | tf_op jit(solution)/shard_map/pallas_call | solution.py:558
  18.8 0.7 %shard_map.87 = (f32[2,4,2,8,128]{4,3,2,1,0:T(8,128)}, f32[4,128]{1,0:T(4,128)}) custom-call(f32[2,4,2,8,128]{4,3,2,1,0:T(8,128)S(1)} %get-tuple-element.4.adjoint, f32[4,128]{1,0:T(4,128)S(1)} %get-tuple-element.5.gradient), custom_call_target="tpu_custom_call" | custom-call | tf_op jit(solution)/shard_map/pallas_call | solution.py:593
